TPU v7x, 128 devices: a whole 4x4x4 slice. The times are simulated.
128 devices in a mesh: dp: 16 (over y_lo, z, core), space: 8 (over y_hi, x).
Axes of the slice: x: 4, y: 4 (y_hi: 2, y_lo: 2; y = y_hi * 2 + y_lo), z: 4, core: 2. Of those that a mesh axis runs over, the one named last changes fastest.
Arguments:
- volume: bfloat16 [16, 32, 32, 32, 128], P('dp', 'space'), may hold values from -6 to 6
- kernel: bfloat16 [3, 3, 3, 128, 256], replicated, may hold values from -0.109375 to 0.109375
- cotangent: bfloat16 [16, 16, 16, 16, 256], P('dp', 'space'), may hold values from -6 to 6
Outputs:
- switched: bfloat16 [16, 256, 4096], P('dp', 'space')
- volume_grad: bfloat16 [16, 32, 32, 32, 128], P('dp', 'space')
- kernel_grad: float32 [3, 3, 3, 128, 256], P(None, None, None, 'dp')
All inputs are finite; a program needn't handle non-finite values.
Results may differ from a plain program's by a relative error of at most 0.0049.
Values may be sent and summed in bfloat16 or wider, within the bound.
A program may use at most 64 MiB of HBM per device.

v0:
```python
import math

import jax
import jax.numpy as jnp
from jax import lax
from jax.sharding import PartitionSpec as P


def from_behind(value, axis, steps):
    count = lax.axis_size(axis)
    first, last = (max(0, -steps), min(count, count - steps))
    return lax.ppermute(value, axis, [(source, source + steps) for source in range(first, last)])


def body(volume, kernel, cotangent):
    below = from_behind(volume[:, -1:], "space", 1)
    extended = jnp.concatenate([below, volume], axis=1)
    preact = lax.conv_general_dilated(
        extended,
        kernel,
        (2, 2, 2),
        ((0, 0), (1, 1), (1, 1)),
        dimension_numbers=("NDHWC", "DHWIO", "NDHWC"),
        preferred_element_type=jnp.float32,
    )
    sigmoid_z = jax.nn.sigmoid(preact)
    activated = (preact * sigmoid_z).astype(jnp.bfloat16)
    slope = sigmoid_z * (1.0 + preact * (1.0 - sigmoid_z))
    grad_pre = (cotangent.astype(jnp.float32) * slope).astype(jnp.bfloat16)
    samples, planes, rows, cols, chans = activated.shape
    channel_major = jnp.transpose(activated, (0, 4, 1, 2, 3)).reshape(
        samples, chans, planes * rows * cols
    )
    switched = lax.all_to_all(channel_major, "space", split_axis=1, concat_axis=2, tiled=True)
    flipped = kernel[::-1, ::-1, ::-1]
    spread = lax.conv_general_dilated(
        grad_pre,
        flipped,
        (1, 1, 1),
        ((2, 2), (1, 2), (1, 2)),
        lhs_dilation=(2, 2, 2),
        dimension_numbers=("NDHWC", "DHWOI", "NDHWC"),
        preferred_element_type=jnp.float32,
    )
    from_upper = from_behind(spread[:, :1], "space", -1)
    data_grad = spread[:, 1:].at[:, -1:].add(from_upper)
    volume_grad = data_grad.astype(jnp.bfloat16)
    kernel_part = lax.conv_general_dilated(
        extended,
        grad_pre,
        (1, 1, 1),
        ((0, 0), (1, 0), (1, 0)),
        rhs_dilation=(2, 2, 2),
        dimension_numbers=("CDHWN", "IDHWO", "DHWNC"),
        preferred_element_type=jnp.float32,
    )
    count = lax.axis_size("dp") * lax.axis_size("space") * planes * rows * cols
    kernel_part = kernel_part * (1.0 / math.sqrt(count))
    summed = lax.psum(kernel_part, "space")
    kernel_grad = lax.psum_scatter(summed, "dp", scatter_dimension=3, tiled=True)
    return (switched, volume_grad, kernel_grad)


def solution(mesh):
    in_specs = (P("dp", "space", None, None, None), P(), P("dp", "space", None, None, None))
    out_specs = (
        P("dp", "space", None),
        P("dp", "space", None, None, None),
        P(None, None, None, "dp", None),
    )
    return jax.shard_map(body, mesh=mesh, in_specs=in_specs, out_specs=out_specs, check_vma=False)
```

profile of v0, /device:TPU:0, one launch (start us, length us, event | category | flops | bytes accessed | tf_op | source)
XLA Modules:
  0.0 215.8 jit_solution(7249158962370149902)
XLA Ops:
  7.2 1.1 slice.58
  8.4 0.6 copy.70
  8.9 3.5 %collective-permute-start = (bf16[1,1,32,32,128]{4,0,3,2,1:T(2,128)(2,1)S(1)}, bf16[1,1,32,32,128]{4,0,3,2,1:T(2,128)(2,1)S(1)}, u32[]{:S(2)}, u32[]{:S(2)}) collective-permute-start(bf16[1,1,32,32,128]{4,0,3,2,1:T(2,128)(2,1)S(1)} %copy.70), channel_id=1, source_target_pairs={{0,1},{1,2},{2,3},{3,4},{4,5},{5,6},{6,7},{8,9},{9,10},{10,11},{11... | collective-permute-start | bytes 786440 | tf_op jit(solution)/shard_map/ppermute | solution.py:12
  12.5 11.1 %collective-permute-done = bf16[1,1,32,32,128]{4,0,3,2,1:T(2,128)(2,1)S(1)} collective-permute-done((bf16[1,1,32,32,128]{4,0,3,2,1:T(2,128)(2,1)S(1)}, bf16[1,1,32,32,128]{4,0,3,2,1:T(2,128)(2,1)S(1)}, u32[]{:S(2)}, u32[]{:S(2)}) %collective-permute-start) | collective-permute-done | bytes 262176 | tf_op jit(solution)/shard_map/ppermute | solution.py:12
  23.6 0.5 constant_dynamic-update-slice_fusion.1
  24.2 2.6 %constant_dynamic-update-slice_fusion = bf16[1,5,32,32,128]{4,0,3,2,1:T(2,128)(2,1)S(1)} fusion(bf16[1,5,32,32,128]{4,0,3,2,1:T(2,128)(2,1)S(1)} %constant_dynamic-update-slice_fusion.1, bf16[1,4,32,32,128]{4,3,2,1,0:T(8,128)(2,1)S(1)} %copy-done.1), kind=kLoop, calls=%fused_computation.34 | loop fusion | bytes 3145728 | tf_op jit(solution)/shard_map/concatenate | solution.py:17
  26.8 1.5 copy.71
  28.3 0.4 pad.2.clone
  28.7 1.3 copy.46
  30.2 2.5 %add_multiply_fusion = (f32[2,16,8,3,256]{4,2,3,1,0:T(8,128)S(1)}, bf16[2,16,8,3,256]{4,2,3,1,0:T(8,128)(2,1)}) fusion(bf16[3,3,3,128,256]{4,3,2,1,0:T(8,128)(2,1)S(1)} %copy-done, bf16[5,32,1,7,2,128]{5,3,4,1,0,2:T(8,128)(2,1)S(1)} %slice.59, bf16[5,32,1,8,6,128]{5,3,4,1,0,2:T(8,128)(2,1)S(1)} %copy.46, pred[8,3]{0,1:T(4,128)(4,1)S(1)} %copy-done.5), kind=kOutput, calls=%fused_computation.16 | convolution fusion | flops 1340473344 | bytes 5488664 | tf_op jit(solution)/shard_map/conv_general_dilated | solution.py:18
  33.1 8.7 %convolution_multiply_fusion = f32[3,3,3,128,256]{4,3,2,1,0:T(8,128)} fusion(bf16[1,5,32,32,128]{4,0,3,2,1:T(2,128)(2,1)S(1)} %constant_dynamic-update-slice_fusion, bf16[1,2,16,16,256]{4,2,3,1,0:T(8,128)(2,1)S(1)} %fusion.21), kind=kOutput, calls=%fused_computation.8 | convolution fusion | flops 869498880 | bytes 5111808 | tf_op jit(solution)/shard_map/conv_general_dilated | solution.py:48
  42.1 0.4 copy-done.2
  42.4 3.9 %convolution_select_fusion = f32[5,32,8,6,128]{4,2,3,1,0:T(8,128)S(1)} fusion(bf16[3,3,3,128,256]{4,3,2,1,0:T(8,128)(2,1)S(1)} %copy-done, pred[8,6]{0,1:T(8,128)(4,1)S(1)} %copy-done.2, bf16[2,16,8,4,256]{4,2,3,1,0:T(8,128)(2,1)S(1)} %fusion.38), kind=kOutput, calls=%fused_computation.10 | convolution fusion | flops 1331625984 | bytes 6225968 | tf_op jit(solution)/shard_map/conv_general_dilated | solution.py:36
  46.3 1.0 fusion.31
  47.6 0.8 slice_bitcast_fusion.1
  48.4 1.3 collective-permute-start.1
  50.0 0.8 copy.48
  50.8 2.0 copy.49
  52.8 0.5 broadcast.77
  53.3 3.8 %reduce.2 = bf16[256,512]{1,0:T(8,128)(2,1)} reduce(bf16[256,1,512]{2,1,0:T(2,128)(2,1)} %bitcast.63, bf16[]{:T(256)} %broadcast.77), dimensions={1}, to_apply=%bitcast.43.reduce_sub_computation | reduce | bytes 524290
  57.1 1.9 reshape.86
  59.0 11.2 %all-to-all-start = ((bf16[8,2,8192]{2,1,0:T(2,128)(2,1)}), bf16[8,2,8192]{2,1,0:T(2,128)(2,1)}, u32[]{:S(2)}, u32[]{:S(2)}) async-start(bf16[8,2,8192]{2,1,0:T(2,128)(2,1)} %reshape.86), calls=%async_computation | async-start | bytes 524288 | tf_op jit(solution)/shard_map/all_to_all | solution.py:34
  70.2 2.3 %copy.56 = f32[1,32,8,6,128]{4,1,3,2,0:T(8,128)} copy(f32[1,32,8,6,128]{4,2,3,1,0:T(8,128)} %get-tuple-element.24) | data formatting | bytes 1572864 | tf_op jit(solution)/shard_map/conv_general_dilated | solution.py:36
  72.5 0.4 copy.55
  73.0 6.1 %all-to-all-done = bf16[8,2,8192]{2,1,0:T(2,128)(2,1)} async-done(((bf16[8,2,8192]{2,1,0:T(2,128)(2,1)}), bf16[8,2,8192]{2,1,0:T(2,128)(2,1)}, u32[]{:S(2)}, u32[]{:S(2)}) %all-to-all-start) | async-done | bytes 262176 | tf_op jit(solution)/shard_map/all_to_all | solution.py:34
  79.0 1.2 reshape.87
  80.3 0.7 copy.64
  81.0 32.9 %reduce-scatter.2.cloned.1.call-done = f32[3,3,3,8,256]{4,3,2,1,0:T(8,128)} async-done(((f32[3,3,3,128,256]{4,3,2,1,0:T(8,128)}), f32[3,3,3,8,256]{4,3,2,1,0:T(8,128)}) %reduce-scatter.2.cloned.1.call-update) | async-done | bytes 221200 | tf_op jit(solution)/shard_map/reduce_scatter | solution.py:60
  114.0 1.3 fusion.17
  115.3 1.4 copy.59
  116.6 90.7 %all-reduce.2.cloned.1.call-done = f32[3,3,3,8,256]{4,3,2,1,0:T(8,128)} async-done(((f32[3,3,3,8,256]{4,3,2,1,0:T(8,128)}), f32[3,3,3,8,256]{4,3,2,1,0:T(8,128)}) %all-reduce.2.cloned.1.call-update) | async-done | bytes 221200 | tf_op jit(solution)/shard_map/psum | solution.py:59
  207.4 1.6 copy.75
  (29 shorter events, 1.6 us)
Async XLA Ops:
  7.2 23.0 %copy-start = (bf16[3,3,3,128,256]{4,3,2,1,0:T(8,128)(2,1)S(1)}, bf16[3,3,3,128,256]{4,3,2,1,0:T(8,128)(2,1)}, u32[]{:S(2)}) copy-start(bf16[3,3,3,128,256]{4,3,2,1,0:T(8,128)(2,1)} %param.6) | copy-start | bytes 5308420
  7.2 17.0 %copy-start.1 = (bf16[1,4,32,32,128]{4,3,2,1,0:T(8,128)(2,1)S(1)}, bf16[1,4,32,32,128]{4,3,2,1,0:T(8,128)(2,1)}, u32[]{:S(2)}) copy-start(bf16[1,4,32,32,128]{4,3,2,1,0:T(8,128)(2,1)} %param.5) | copy-start | bytes 3145732
  7.2 106.7 %reduce-scatter.2.cloned.1.call-start = ((), (), s32[]{:S(2)}) async-start(), calls=%async_computation.2 | async-start | bytes 3760128 | tf_op jit(solution)/shard_map/reduce_scatter | solution.py:60
  8.9 14.7 %collective-permute-start = (bf16[1,1,32,32,128]{4,0,3,2,1:T(2,128)(2,1)S(1)}, bf16[1,1,32,32,128]{4,0,3,2,1:T(2,128)(2,1)S(1)}, u32[]{:S(2)}, u32[]{:S(2)}) collective-permute-start(bf16[1,1,32,32,128]{4,0,3,2,1:T(2,128)(2,1)S(1)} %copy.70), channel_id=1, source_target_pairs={{0,1},{1,2},{2,3},{3,4},{4,5},{5,6},{6,7},{8,9},{9,10},{10,11},{11... | collective-permute-start | bytes 786440 | tf_op jit(solution)/shard_map/ppermute | solution.py:12
  28.7 1.5 copy-start.5
  30.2 2.7 %copy-start.4 = (bf16[1,2,16,16,256]{4,3,2,1,0:T(8,128)(2,1)S(1)}, bf16[1,2,16,16,256]{4,3,2,1,0:T(8,128)(2,1)}, u32[]{:S(2)}) copy-start(bf16[1,2,16,16,256]{4,3,2,1,0:T(8,128)(2,1)} %param.7) | copy-start | bytes 786436
  41.8 0.7 copy-start.2
  47.3 2.6 %copy-start.3 = (bf16[2,16,8,3,256]{4,2,3,1,0:T(8,128)(2,1)S(1)}, bf16[2,16,8,3,256]{4,2,3,1,0:T(8,128)(2,1)}, u32[]{:S(2)}) copy-start(bf16[2,16,8,3,256]{4,2,3,1,0:T(8,128)(2,1)} %get-tuple-element.27) | copy-start | bytes 1179652
  48.4 65.6 %collective-permute-start.1 = (f32[1,1,32,32,128]{4,2,3,1,0:T(8,128)}, f32[1,1,32,32,128]{4,2,3,1,0:T(8,128)}, u32[]{:S(2)}, u32[]{:S(2)}) collective-permute-start(f32[1,1,32,32,128]{4,2,3,1,0:T(8,128)} %slice_bitcast_fusion.1), channel_id=1, source_target_pairs={{1,0},{2,1},{3,2},{4,3},{5,4},{6,5},{7,6},{9,8},{10,9},{11,10},{12... | collective-permute-start | bytes 1572872 | tf_op jit(solution)/shard_map/ppermute | solution.py:12
  59.0 20.1 %all-to-all-start = ((bf16[8,2,8192]{2,1,0:T(2,128)(2,1)}), bf16[8,2,8192]{2,1,0:T(2,128)(2,1)}, u32[]{:S(2)}, u32[]{:S(2)}) async-start(bf16[8,2,8192]{2,1,0:T(2,128)(2,1)} %reshape.86), calls=%async_computation | async-start | bytes 524288 | tf_op jit(solution)/shard_map/all_to_all | solution.py:34
  70.1 137.2 %all-reduce.2.cloned.1.call-start = ((), (), s32[]{:S(2)}) async-start(), calls=%async_computation.3 | async-start | bytes 442368 | tf_op jit(solution)/shard_map/psum | solution.py:59
Sparse Core Ops, SparseCore 0:
  41.9 71.9 reduce-scatter.1
  116.4 90.9 all-reduce.1
where the time goes:
time: 216 us
  waiting for transfers between devices  141 us (65%)
  local copies, waits for them, and re-layouts  24.2 us (11%)
  starting transfers between devices  16.1 us (7%)
  matrix products  15 us (7%)
  between operations  14.3 us (7%)
  other arithmetic  5.35 us (2%)
    psum x1, waiting for transfers between devices, body(): summed = lax.psum(kernel_part, 'space')  90.7 us
    reduce_scatter x1, waiting for transfers between devices, body(): lax.psum_scatter(summed, 'dp', scatter_dimension=3, tiled=True)  32.9 us
    all_to_all x1, starting transfers between devices, body(): lax.all_to_all(channel_major, 'space', split_axis=1, concat_axis=2, tiled...  11.2 us
    ppermute x2, waiting for transfers between devices, from_behind(): lax.ppermute(value, axis, [(source, source + steps) for source in range(f...  11.1 us
    unnamed x21, local copies, waits for them, and re-layouts  9.65 us
    conv_general_dilated x1, matrix products, body(): lax.conv_general_dilated(extended, grad_pre, (1, 1, 1), ((0, 0), (1, 0),...  8.67 us
    all_to_all x1, waiting for transfers between devices, body(): lax.all_to_all(channel_major, 'space', split_axis=1, concat_axis=2, tiled...  6.08 us
    ppermute x2, starting transfers between devices, from_behind(): lax.ppermute(value, axis, [(source, source + steps) for source in range(f...  4.82 us
  transfers between devices with their start and end apart: 5, of which 4 were waited for; matrix products, arithmetic and copies ran while one was open for 11% of the time, Pallas kernels for 0%

commit v1 on v0

v1 whole, which is shorter than its diff:
```python
import functools

import jax
import jax.numpy as jnp
from jax import lax
from jax.experimental import pallas as pl
from jax.experimental.pallas import tpu as pltpu
from jax.sharding import PartitionSpec as P

MESH = pl.DeviceIdType.MESH
BF, F32 = jnp.bfloat16, jnp.float32
NT = (((1,), (1,)), ((), ()))
TAPS = 9
PAIRS = {0: ((1, 1), (3, 2)), 1: ((0, 0), (2, 1)), 2: ((1, 0), (3, 1))}
REACH = {0: ((0, 1),), 1: ((0, 2), (1, 0)), 2: ((1, 1),), 3: ((1, 2), (2, 0))}


def nt(a, b):
    return lax.dot_general(a, b, NT, preferred_element_type=F32)


def mm(a, b):
    return jnp.dot(a, b, preferred_element_type=F32)


def kernel(
    scale,
    vol_hbm, w_hbm, ct_hbm,
    sw_ref, vg_ref, kg_ref,
    vol, w, ct, spread, taps, tt, ttr, gp, gps, gpr, hs, hr, swb, fine,
    o1, w1, c1, o2, w2, c2, o3, w3, c3,
    in_sem, pair_ss, pair_rs, halo_ss, halo_rs, sw_ss, sw_rs, red_ss, red_rs,
):
    dp, sp = lax.axis_index("dp"), lax.axis_index("space")
    core, z, y, x = dp % 2, (dp // 2) % 4, (sp // 4) * 2 + dp // 8, sp % 4

    def chip(x, y, z, core):
        return ((y % 2) * 8 + z * 2 + core, (y // 2) * 4 + x)

    partner = chip(x, y, z, 1 - core)
    along = {
        "z": [chip(x, y, (z + j) % 4, core) for j in (1, 2, 3)],
        "y": [chip(x, (y + j) % 4, z, core) for j in (1, 2, 3)],
        "x": [chip((x + j) % 4, y, z, core) for j in (1, 2, 3)],
    }
    slabs = [(dp, (sp + j) % 8) for j in range(1, 8)]

    def remote(src, dst, ss, rs, to):
        return pltpu.make_async_remote_copy(
            src_ref=src, dst_ref=dst, send_sem=ss, recv_sem=rs, device_id=to, device_id_type=MESH
        )

    loads = {}
    for i, p in enumerate((3, 1, 2, 0)):
        loads["v", p] = pltpu.make_async_copy(vol_hbm.at[p], vol.at[p], in_sem.at[i])
    for kd in range(3):
        rows = pl.ds(kd * 1152, 1152)
        loads["w", kd] = pltpu.make_async_copy(w_hbm.at[rows], w.at[rows], in_sem.at[4 + kd])
    loads["c"] = pltpu.make_async_copy(ct_hbm, ct, in_sem.at[7])
    for which in (("v", 3), ("w", 0), ("v", 1), ("v", 2), ("w", 1), ("w", 2), ("v", 0), "c"):
        loads[which].start()

    barrier = pltpu.get_barrier_semaphore()
    peers = [partner, *along["z"], along["y"][0], along["y"][2], *slabs]
    for peer in peers:
        pl.semaphore_signal(barrier, inc=1, device_id=peer, device_id_type=MESH)

    def edge(condition, ref):
        @pl.when(condition)
        def _():
            ref[...] = jnp.zeros(ref.shape, ref.dtype)

    edge(sp == 7, gp.at[2])
    edge(sp == 0, hr)

    first_column = lax.broadcasted_iota(jnp.int32, (512, 128), 0) % 16 == 0
    last_column = lax.broadcasted_iota(jnp.int32, (256, 256), 0) % 16 == 15

    def unfold(p):
        loads["v", p].wait()
        spread[pl.ds(8, 1024)] = vol[p].astype(F32)
        even = spread[pl.ds(8, 512, stride=2)].astype(BF)
        odd = spread[pl.ds(9, 512, stride=2)].astype(BF)
        left = jnp.where(first_column, 0.0, spread[pl.ds(7, 512, stride=2)]).astype(BF)
        for kw, source in enumerate((left, even, odd)):
            rows = source.reshape(16, 32, 128)
            upper, lower = rows[:, :16], rows[:, 16:]
            before = jnp.concatenate([jnp.zeros((1, 16, 128), BF), lower[:-1]], axis=0)
            for kh, block in enumerate((before, upper, lower)):
                at = (kh * 3 + kw) * 128
                taps[p, :, at : at + 128] = block.reshape(256, 128)

    row = lax.broadcasted_iota(jnp.int32, (128, 128), 0)
    column = lax.broadcasted_iota(jnp.int32, (128, 128), 1)
    channel = (((row % 64) // 8) * 2 + row // 64) * 8 + row % 8
    sort = (column == channel).astype(F32).astype(BF)

    def turn(p):
        for t in range(TAPS):
            turned = nt(sort, taps[p, :, t * 128 : (t + 1) * 128]).astype(BF)
            tt[0, p, t * 64 : (t + 1) * 64] = turned[:64]
            tt[1, p, t * 64 : (t + 1) * 64] = turned[64:]

    spread[0:8] = jnp.zeros((8, 128), F32)
    unfold(3)
    loads["w", 0].wait()
    hs[...] = mm(taps[3], w[0:1152]).astype(BF)
    pl.semaphore_wait(barrier, len(peers))
    halo = remote(hs, hr, halo_ss.at[0], halo_rs.at[0], (dp, (sp + 1) % 8))

    @pl.when(sp < 7)
    def _():
        halo.start()

    unfold(1)
    unfold(2)
    loads["w", 1].wait()
    loads["w", 2].wait()
    pre1 = mm(taps[1], w[0:1152]) + mm(taps[2], w[1152:2304]) + mm(taps[3], w[2304:3456])

    er = lax.broadcasted_iota(jnp.int32, (256, 256), 0)
    ec = lax.broadcasted_iota(jnp.int32, (256, 256), 1)
    unit = (er == ec).astype(F32).astype(BF)

    def share(o):
        return remote(gp.at[o], gpr.at[o], pair_ss.at[4 + o], pair_rs.at[4 + o], partner)

    def to_right(o):
        value = gp[o].astype(F32)
        gps[o] = jnp.where(last_column, 0.0, pltpu.roll(value, 255, 0)).astype(BF)

    def finish(o, v):
        s = jax.nn.sigmoid(v)
        slope = s * (1.0 + v * (1.0 - s))
        rows = pl.ds(o * 256, 256)
        gp[o] = (ct[rows].astype(F32) * slope).astype(BF)
        return (v * s).astype(BF)

    loads["c"].wait()
    act1 = finish(1, pre1)
    share(1).start()
    to_right(1)

    unfold(0)
    pre0 = mm(taps[0], w[1152:2304]) + mm(taps[1], w[2304:3456])
    pairs = []
    for p in (0, 1, 2, 3):
        turn(p)
        pairs.append(remote(tt.at[1 - core, p], ttr.at[p], pair_ss.at[p], pair_rs.at[p], partner))
        pairs[-1].start()
    swb[:, 256:512] = nt(unit, act1).astype(BF)

    def grad_plane(p):
        for half, moves in ((0, ((1, 0),)), (1, ((2, 0), (0, 1)))):
            lhs, lhs_right, rhs, rhs_right = [], [], [], []
            for o, kd in REACH[p]:
                for kh, down in moves:
                    for source, out in ((gp, lhs), (gps, lhs_right)):
                        value = source[o]
                        if down:
                            value = jnp.concatenate([value[16:], jnp.zeros((16, 256), BF)], axis=0)
                        out.append(value)
                    at = (kd * 9 + kh * 3) * 128
                    rhs_right.append(w[at : at + 128])
                    rhs.append(w[at + 128 : at + 384])
            both = nt(jnp.concatenate(lhs, axis=1), jnp.concatenate(rhs, axis=1))
            more = nt(jnp.concatenate(lhs_right, axis=1), jnp.concatenate(rhs_right, axis=1))
            fine[:, pl.ds(half * 32, 16, stride=2), :] = both[:, :128].reshape(16, 16, 128)
            fine[:, pl.ds(half * 32 + 1, 16, stride=2), :] = (both[:, 128:] + more).reshape(16, 16, 128)
        vg_ref[p] = fine[...].reshape(1024, 128).astype(BF)

    grad_plane(2)

    @pl.when(sp > 0)
    def _():
        halo.wait_recv()

    act0 = finish(0, pre0 + hr[...].astype(F32))
    share(0).start()
    back = remote(gp.at[0], gp.at[2], halo_ss.at[1], halo_rs.at[1], (dp, (sp + 7) % 8))

    @pl.when(sp > 0)
    def _():
        back.start()

    def own_part(kd):
        (a, oa), (b, ob) = PAIRS[kd]
        lhs = jnp.concatenate([tt[core, a], tt[core, b]], axis=1)
        return mm(lhs, jnp.concatenate([gp[oa], gp[ob]], axis=0))

    def pair_part(kd):
        (a, oa), (b, ob) = PAIRS[kd]
        lhs = jnp.concatenate([ttr[a], ttr[b]], axis=1)
        return mm(lhs, jnp.concatenate([gpr[oa], gpr[ob]], axis=0))

    def put1(kd, total):
        for t in range(TAPS):
            for group in range(8):
                block = total[t * 64 + group * 8 : t * 64 + group * 8 + 8]
                tile = jnp.concatenate([block[:, :128], block[:, 128:]], axis=0)
                o1[kd, group % 4, (group // 4) * 9 + t] = tile
                w1[kd, group % 4, (group // 4) * 9 + t] = tile.astype(BF)

    def copies(kd, stage):
        out = []
        for j in range(3):
            at = (kd * 3 + stage) * 3 + j
            if stage == 0:
                src, dst, to = w1.at[kd, (z + j + 1) % 4], c1.at[kd, j], along["z"][j]
            elif stage == 1:
                src, dst, to = w2.at[kd, (y + j + 1) % 2], c2.at[kd, j], along["y"][j]
            else:
                src, dst, to = w3.at[kd], c3.at[kd, j], along["x"][j]
            out.append(remote(src, dst, red_ss.at[at], red_rs.at[at], to))
        return out

    def send(kd, stage):
        for c in copies(kd, stage):
            c.start()

    def arrive(kd, stage):
        for c in copies(kd, stage):
            c.wait_recv()

    def summed(own, got):
        return own + got[0].astype(F32) + got[1].astype(F32) + got[2].astype(F32)

    def step1(kd):
        arrive(kd, 0)
        total = summed(o1[kd, z], c1.at[kd]).reshape(2, 9, 16, 128)
        o2[kd] = total
        w2[kd] = total.astype(BF)
        send(kd, 1)

    def step2(kd):
        arrive(kd, 1)
        total = summed(o2[kd, y % 2], c2.at[kd])
        o3[kd] = total
        w3[kd] = total.astype(BF)
        send(kd, 2)

    def step3(kd):
        arrive(kd, 2)
        total = summed(o3[kd], c3.at[kd]) * scale
        for t in range(TAPS):
            at = (kd * 9 + t) * 8
            kg_ref[at : at + 8, 0:128] = total[t, 0:8]
            kg_ref[at : at + 8, 128:256] = total[t, 8:16]

    part1, part2 = own_part(1), own_part(2)
    for c in pairs:
        c.wait_recv()
    share(1).wait_recv()
    share(0).wait_recv()
    put1(1, part1 + pair_part(1))
    send(1, 0)
    put1(2, part2 + pair_part(2))
    send(2, 0)

    swb[:, 0:256] = nt(unit, act0).astype(BF)
    columns = pl.ds(pl.multiple_of(sp * 512, 512), 512)
    switches = []
    for j, to in enumerate(slabs):
        rows = pl.ds(pl.multiple_of(to[1] * 32, 32), 32)
        switches.append(remote(swb.at[rows], sw_ref.at[:, columns], sw_ss.at[j], sw_rs.at[j], to))
        switches[-1].start()
    sw_ref[:, columns] = swb[pl.ds(pl.multiple_of(sp * 32, 32), 32)]
    to_right(0)
    grad_plane(0)

    @pl.when(sp < 7)
    def _():
        back.wait_recv()

    share(2).start()
    part0 = own_part(0)
    step1(1)
    share(2).wait_recv()
    put1(0, part0 + pair_part(0))
    send(0, 0)
    step1(2)
    to_right(2)
    grad_plane(1)
    step2(1)
    step2(2)
    grad_plane(3)
    step1(0)
    step3(1)
    step2(0)
    step3(2)
    step3(0)

    for c in switches:
        c.wait()
    for c in pairs:
        c.wait_send()
    for o in range(3):
        share(o).wait_send()
    for kd in range(3):
        for stage in range(3):
            for c in copies(kd, stage):
                c.wait_send()

    @pl.when(sp < 7)
    def _():
        halo.wait_send()

    @pl.when(sp > 0)
    def _():
        back.wait_send()


def body(volume, weights, cotangent):
    count = 16 * 16 * 16 * 16
    vmem = functools.partial(pltpu.VMEM)
    dma = pltpu.SemaphoreType.DMA
    whole = pl.BlockSpec(memory_space=pltpu.VMEM)
    switched, volume_grad, kernel_grad = pl.pallas_call(
        functools.partial(kernel, 1.0 / count**0.5),
        out_shape=(
            jax.ShapeDtypeStruct((32, 4096), BF),
            jax.ShapeDtypeStruct((4, 1024, 128), BF),
            jax.ShapeDtypeStruct((216, 256), F32),
        ),
        in_specs=[pl.BlockSpec(memory_space=pl.ANY)] * 3,
        out_specs=(whole, whole, whole),
        scratch_shapes=[
            vmem((4, 1024, 128), BF),
            vmem((3456, 256), BF),
            vmem((512, 256), BF),
            vmem((1040, 128), F32),
            vmem((4, 256, 1152), BF),
            vmem((2, 4, 576, 256), BF),
            vmem((4, 576, 256), BF),
            vmem((3, 256, 256), BF),
            vmem((3, 256, 256), BF),
            vmem((3, 256, 256), BF),
            vmem((256, 256), BF),
            vmem((256, 256), BF),
            vmem((256, 512), BF),
            vmem((16, 64, 128), F32),
            vmem((3, 4, 18, 16, 128), F32),
            vmem((3, 4, 18, 16, 128), BF),
            vmem((3, 3, 18, 16, 128), BF),
            vmem((3, 2, 9, 16, 128), F32),
            vmem((3, 2, 9, 16, 128), BF),
            vmem((3, 3, 9, 16, 128), BF),
            vmem((3, 9, 16, 128), F32),
            vmem((3, 9, 16, 128), BF),
            vmem((3, 3, 9, 16, 128), BF),
            dma((8,)),
            dma((7,)),
            dma((7,)),
            dma((2,)),
            dma((2,)),
            dma((7,)),
            dma((7,)),
            dma((27,)),
            dma((27,)),
        ],
        compiler_params=pltpu.CompilerParams(
            collective_id=0, has_side_effects=True, vmem_limit_bytes=56 * 2**20
        ),
        name="conv_step",
    )(
        volume.reshape(4, 1024, 128),
        weights.reshape(3456, 256),
        cotangent.reshape(512, 256),
    )
    return (
        switched[None],
        volume_grad.reshape(1, 4, 32, 32, 128),
        kernel_grad.reshape(3, 3, 3, 8, 256),
    )


def solution(mesh):
    in_specs = (P("dp", "space", None, None, None), P(), P("dp", "space", None, None, None))
    out_specs = (
        P("dp", "space", None),
        P("dp", "space", None, None, None),
        P(None, None, None, "dp", None),
    )
    return jax.shard_map(body, mesh=mesh, in_specs=in_specs, out_specs=out_specs, check_vma=False)
```

time: 216 us -> 43.8 us (0.20)
  waiting for transfers between devices: 141 us -> 0 us
  Pallas kernels: 0 us -> 38.3 us
  local copies, waits for them, and re-layouts: 24.2 us -> 4.68 us
  starting transfers between devices: 16.1 us -> 0 us
  matrix products: 15 us -> 0 us
  between operations: 14.3 us -> 0.65 us
  other arithmetic: 5.35 us -> 0 us
    psum x1 -> x0, waiting for transfers between devices: 90.7 us -> none  [body(): summed = lax.psum(kernel_part, 'space')]
    pallas_call x0 -> x1, Pallas kernels: none -> 38.3 us  [body(): pl.pallas_call(functools.partial(kernel, 1.0 / count ** 0.5), out_shape=(...]
    reduce_scatter x1 -> x0, waiting for transfers between devices: 32.9 us -> none  [body(): lax.psum_scatter(summed, 'dp', scatter_dimension=3, tiled=True)]
    conv_general_dilated x3 -> x0, matrix products: 15 us -> none  [the longest x1 8.67 us: body(): lax.conv_general_dilated(extended, grad_pre, (1, 1, 1), ((0, 0), (1, 0),...]
    all_to_all x1 -> x0, starting transfers between devices: 11.2 us -> none  [body(): lax.all_to_all(channel_major, 'space', split_axis=1, concat_axis=2, tiled...]
    ppermute x2 -> x0, waiting for transfers between devices: 11.1 us -> none  [from_behind(): lax.ppermute(value, axis, [(source, source + steps) for source in range(f...]
    all_to_all x1 -> x0, waiting for transfers between devices: 6.08 us -> none  [body(): lax.all_to_all(channel_major, 'space', split_axis=1, concat_axis=2, tiled...]
    conv_general_dilated x9 -> x0, local copies, waits for them, and re-layouts: 5.74 us -> none  [the longest x7 4.3 us: body(): lax.conv_general_dilated(grad_pre, flipped, (1, 1, 1), ((2, 2), (1, 2), (...]
  transfers between devices with their start and end apart: 5 -> 0, of which waited for: 4 -> 0; matrix products, arithmetic and copies ran while one was open for 11% -> 0% of each run, Pallas kernels for 0% -> 0%
where the time goes in v1:
time: 43.8 us; the launch traced here: 43.7 us
  Pallas kernels  38.3 us (87%)
  local copies, waits for them, and re-layouts  4.68 us (11%)
  between operations  0.65 us (1%)
    pallas_call x1, Pallas kernels, body(): pl.pallas_call(functools.partial(kernel, 1.0 / count ** 0.5), out_shape=(...  38.3 us
    unnamed x5, local copies, waits for them, and re-layouts  4.68 us

profile of v1, /device:TPU:0, one launch (start us, length us, event | category | flops | bytes accessed | tf_op | source)
XLA Modules:
  0.0 43.7 jit_solution(16101600109705208640)
XLA Ops:
  0.6 38.3 %conv_step.1 = (bf16[32,4096]{1,0:T(8,128)(2,1)}, bf16[4,1024,128]{2,1,0:T(8,128)(2,1)}, f32[216,256]{1,0:T(8,128)}) custom-call(bf16[4,1024,128]{2,1,0:T(8,128)(2,1)} %bitcast.7, bf16[3456,256]{1,0:T(8,128)(2,1)} %bitcast.6, bf16[512,256]{1,0:T(8,128)(2,1)} %bitcast.9), custom_call_target="tpu_custom_call" | custom-call | tf_op jit(solution)/shard_map/conv_step/pallas_call | solution.py:318
  39.0 0.0 copy-start
  39.0 1.7 %copy.9 = bf16[1,32,4096]{2,1,0:T(8,128)(2,1)} copy(bf16[1,32,4096]{2,1,0:T(8,128)(2,1)} %bitcast.10) | data formatting | bytes 524288
  40.7 2.3 %copy.10 = bf16[1,4,32,32,128]{4,3,2,1,0:T(8,128)(2,1)} copy(bf16[1,4,32,32,128]{4,3,2,1,0:T(8,128)(2,1)} %bitcast.8) | data formatting | bytes 2097152
  43.0 0.0 copy-done
  43.0 0.7 %copy.11 = f32[3,3,3,8,256]{4,3,2,1,0:T(8,128)} copy(f32[3,3,3,8,256]{4,3,2,1,0:T(8,128)S(1)} %bitcast.11) | data formatting | bytes 442368
Async XLA Ops:
  39.0 4.0 %copy-start = (f32[216,256]{1,0:T(8,128)S(1)}, f32[216,256]{1,0:T(8,128)}, u32[]{:S(2)}) copy-start(f32[216,256]{1,0:T(8,128)} %get-tuple-element.8) | copy-start | bytes 663556

commit v2 on v1

v2 whole, which is shorter than its diff:
```python
import functools

import jax
import jax.numpy as jnp
from jax import lax
from jax.experimental import pallas as pl
from jax.experimental.pallas import tpu as pltpu
from jax.sharding import PartitionSpec as P

MESH = pl.DeviceIdType.MESH
BF, F32 = jnp.bfloat16, jnp.float32
NT = (((1,), (1,)), ((), ()))
TAPS = 9
PAIRS = {0: ((1, 1), (3, 2)), 1: ((0, 0), (2, 1)), 2: ((1, 0), (3, 1))}
REACH = {0: ((0, 1),), 1: ((0, 2), (1, 0)), 2: ((1, 1),), 3: ((1, 2), (2, 0))}


def nt(a, b):
    return lax.dot_general(a, b, NT, preferred_element_type=F32)


def mm(a, b):
    return jnp.dot(a, b, preferred_element_type=F32)


class Part:
    def __init__(self, kd, low, count, order):
        self.kd, self.low, self.count, self.order = kd, low, count, order
        self.half = (count + 1) // 2
        if order == "z":
            self.sizes = ((4, 2 * count), (2, count), (1, count))
        else:
            self.sizes = ((4, 4 * self.half), (4, self.half), (1, self.half))
        self.copies = 9 if order == "z" else 10

    def scratch(self):
        shapes = []
        for blocks, tiles in self.sizes:
            shapes.append(pltpu.VMEM((blocks, tiles, 16, 128), F32))
            shapes.append(pltpu.VMEM((blocks, tiles, 16, 128), BF))
            shapes.append(pltpu.VMEM((3, tiles, 16, 128), BF))
        if self.order == "y":
            shapes += [pltpu.VMEM((self.half, 16, 128), F32)] * 2
        return shapes


PARTS = (Part(1, 0, 9, "z"), Part(2, 0, 9, "y"), Part(0, 0, 5, "z"), Part(0, 5, 4, "y"))
SUMS = sum(part.copies for part in PARTS)


def kernel(scale, vol_hbm, w_hbm, ct_hbm, sw_ref, vg_ref, kg_ref, *rest):
    (
        vol, w, ct, spread, taps, tt, ttr, gp, gps, gpr, hs, hr, ps, pr, cr, swb, fine,
        in_sem, pair_ss, pair_rs, edge_ss, edge_rs, sw_ss, sw_rs, sum_ss, sum_rs, ready,
    ) = rest[:27]
    rest, room, number = list(rest[27:]), {}, {}
    for i, part in enumerate(PARTS):
        count = len(part.scratch())
        room[i], rest = rest[:count], rest[count:]
        number[i] = sum(p.copies for p in PARTS[:i])

    dp, sp = lax.axis_index("dp"), lax.axis_index("space")
    core, z, y, x = dp % 2, (dp // 2) % 4, (sp // 4) * 2 + dp // 8, sp % 4
    y_hi = sp // 4

    def chip(x, y, z, core):
        return ((y % 2) * 8 + z * 2 + core, (y // 2) * 4 + x)

    partner = chip(x, y, z, 1 - core)
    along = {
        "z": [chip(x, y, (z + j) % 4, core) for j in (1, 2, 3)],
        "y": [chip(x, (y + j) % 4, z, core) for j in (1, 2, 3)],
        "x": [chip((x + j) % 4, y, z, core) for j in (1, 2, 3)],
    }
    slabs = [(dp, (sp + j) % 8) for j in range(1, 8)]
    above, below = (dp, (sp + 1) % 8), (dp, (sp + 7) % 8)

    def remote(src, dst, ss, rs, to):
        return pltpu.make_async_remote_copy(
            src_ref=src, dst_ref=dst, send_sem=ss, recv_sem=rs, device_id=to, device_id_type=MESH
        )

    def signal(sem, to):
        pl.semaphore_signal(sem, inc=1, device_id=to, device_id_type=MESH)

    loads = {}
    for i, p in enumerate((3, 0, 1, 2)):
        loads["v", p] = pltpu.make_async_copy(vol_hbm.at[p], vol.at[p], in_sem.at[i])
    for kd in range(3):
        rows = pl.ds(kd * 1152, 1152)
        loads["w", kd] = pltpu.make_async_copy(w_hbm.at[rows], w.at[rows], in_sem.at[4 + kd])
    loads["c"] = pltpu.make_async_copy(ct_hbm, ct, in_sem.at[7])
    for which in (("v", 3), ("w", 0), ("v", 0), ("v", 1), ("w", 1), ("w", 2), ("v", 2), "c"):
        loads[which].start()

    barrier = pltpu.get_barrier_semaphore()
    near = [along[axis][j] for axis in "xyz" for j in (0, 2)]
    for peer in [partner, *near]:
        signal(barrier, peer)

    @pl.when(sp == 3)
    def _():
        signal(barrier, above)

    @pl.when(sp == 4)
    def _():
        signal(barrier, below)

    def edge(condition, ref):
        @pl.when(condition)
        def _():
            ref[...] = jnp.zeros(ref.shape, ref.dtype)

    edge(sp == 7, gp.at[2])
    edge(sp == 0, hr)

    first_column = lax.broadcasted_iota(jnp.int32, (512, 128), 0) % 16 == 0
    last_column = lax.broadcasted_iota(jnp.int32, (256, 256), 0) % 16 == 15

    def unfold(p):
        loads["v", p].wait()
        spread[pl.ds(8, 1024)] = vol[p].astype(F32)
        even = spread[pl.ds(8, 512, stride=2)].astype(BF)
        odd = spread[pl.ds(9, 512, stride=2)].astype(BF)
        left = jnp.where(first_column, 0.0, spread[pl.ds(7, 512, stride=2)]).astype(BF)
        for kw, source in enumerate((left, even, odd)):
            rows = source.reshape(16, 32, 128)
            upper, lower = rows[:, :16], rows[:, 16:]
            before = jnp.concatenate([jnp.zeros((1, 16, 128), BF), lower[:-1]], axis=0)
            for kh, block in enumerate((before, upper, lower)):
                at = (kh * 3 + kw) * 128
                taps[p, :, at : at + 128] = block.reshape(256, 128)

    row = lax.broadcasted_iota(jnp.int32, (128, 128), 0)
    column = lax.broadcasted_iota(jnp.int32, (128, 128), 1)
    channel = (((row % 64) // 8) * 2 + row // 64) * 8 + row % 8
    sort = (column == channel).astype(F32).astype(BF)
    pairs = []

    def turn(p):
        for t in range(TAPS):
            turned = nt(sort, taps[p, :, t * 128 : (t + 1) * 128]).astype(BF)
            tt[0, p, t * 64 : (t + 1) * 64] = turned[:64]
            tt[1, p, t * 64 : (t + 1) * 64] = turned[64:]
        pairs.append(remote(tt.at[1 - core, p], ttr.at[p], pair_ss.at[p], pair_rs.at[p], partner))
        pairs[-1].start()

    er = lax.broadcasted_iota(jnp.int32, (256, 256), 0)
    ec = lax.broadcasted_iota(jnp.int32, (256, 256), 1)
    unit = (er == ec).astype(F32).astype(BF)

    def share(o):
        return remote(gp.at[o], gpr.at[o], pair_ss.at[4 + o], pair_rs.at[4 + o], partner)

    def to_right(o):
        value = gp[o].astype(F32)
        gps[o] = jnp.where(last_column, 0.0, pltpu.roll(value, 255, 0)).astype(BF)

    def slope_of(v):
        s = jax.nn.sigmoid(v)
        return s, s * (1.0 + v * (1.0 - s))

    def finish(o, v):
        s, slope = slope_of(v)
        gp[o] = (ct[pl.ds(o * 256, 256)].astype(F32) * slope).astype(BF)
        swb[:, o * 256 : (o + 1) * 256] = nt(unit, (v * s).astype(BF)).astype(BF)

    def grad_plane(p):
        for half, moves in ((0, ((1, 0),)), (1, ((2, 0), (0, 1)))):
            lhs, lhs_right, rhs, rhs_right = [], [], [], []
            for o, kd in REACH[p]:
                for kh, down in moves:
                    for source, out in ((gp, lhs), (gps, lhs_right)):
                        value = source[o]
                        if down:
                            value = jnp.concatenate([value[16:], jnp.zeros((16, 256), BF)], axis=0)
                        out.append(value)
                    at = (kd * 9 + kh * 3) * 128
                    rhs_right.append(w[at : at + 128])
                    rhs.append(w[at + 128 : at + 384])
            both = nt(jnp.concatenate(lhs, axis=1), jnp.concatenate(rhs, axis=1))
            more = nt(jnp.concatenate(lhs_right, axis=1), jnp.concatenate(rhs_right, axis=1))
            fine[:, pl.ds(half * 32, 16, stride=2), :] = both[:, :128].reshape(16, 16, 128)
            fine[:, pl.ds(half * 32 + 1, 16, stride=2), :] = (both[:, 128:] + more).reshape(16, 16, 128)
        vg_ref[p] = fine[...].reshape(1024, 128).astype(BF)

    def own_part(kd):
        (a, oa), (b, ob) = PAIRS[kd]
        lhs = jnp.concatenate([tt[core, a], tt[core, b]], axis=1)
        return mm(lhs, jnp.concatenate([gp[oa], gp[ob]], axis=0))

    def pair_part(kd):
        (a, oa), (b, ob) = PAIRS[kd]
        lhs = jnp.concatenate([ttr[a], ttr[b]], axis=1)
        return mm(lhs, jnp.concatenate([gpr[oa], gpr[ob]], axis=0))

    def copies(i, stage):
        part, refs, out = PARTS[i], room[i], []
        if stage == 3:
            at = number[i] + 9
            return [remote(refs[9], refs[10], sum_ss.at[at], sum_rs.at[at], along["y"][1])]
        axis = ("zyx" if part.order == "z" else "yzx")[stage]
        mine = {"z": z, "y": y, "x": 0}[axis]
        blocks = part.sizes[stage][0]
        for j in range(3):
            at = number[i] + stage * 3 + j
            src = refs[3 * stage + 1].at[(mine + j + 1) % blocks]
            out.append(remote(src, refs[3 * stage + 2].at[j], sum_ss.at[at], sum_rs.at[at], along[axis][j]))
        return out

    def send(i, stage):
        for c in copies(i, stage):
            c.start()

    def put(i, total):
        part, refs = PARTS[i], room[i]

        def store(block, tile_at, tile):
            refs[0][block, tile_at] = tile
            refs[1][block, tile_at] = tile.astype(BF)

        for t in range(part.count):
            for group in range(8):
                at = (part.low + t) * 64 + group * 8
                tile = jnp.concatenate([total[at : at + 8, :128], total[at : at + 8, 128:]], axis=0)
                y_lo, to_z = group // 4, group % 4
                if part.order == "z":
                    store(to_z, y_lo * part.count + t, tile)
                else:
                    for upper in range(2):
                        k = t - upper * (part.count - part.half)
                        if 0 <= k < part.half:
                            store(upper * 2 + y_lo, to_z * part.half + k, tile)
        send(i, 0)

    def write(part, start, count, value):
        for t in range(count):
            at = pl.multiple_of((part.kd * 9 + part.low + start + t) * 8, 8)
            kg_ref[pl.ds(at, 8), 0:128] = value[t, 0:8]
            kg_ref[pl.ds(at, 8), 128:256] = value[t, 8:16]

    def step(i, stage):
        part, refs = PARTS[i], room[i]
        for c in copies(i, stage):
            c.wait_recv()
        if stage == 3:
            write(part, (1 - y_hi) * (part.count - part.half), part.half, refs[10][...])
            return
        own, _, got = refs[3 * stage : 3 * stage + 3]
        axis = ("zyx" if part.order == "z" else "yzx")[stage]
        mine = {"z": z, "y": y, "x": 0}[axis]
        total = own[mine % part.sizes[stage][0]]
        for j in range(3):
            total = total + got[j].astype(F32)
        if stage < 2:
            total = total.reshape(*part.sizes[stage + 1], 16, 128)
            refs[3 * stage + 3][...] = total
            refs[3 * stage + 4][...] = total.astype(BF)
            send(i, stage + 1)
        elif part.order == "z":
            write(part, 0, part.count, total * scale)
        else:
            refs[9][...] = total * scale
            send(i, 3)
            write(part, y_hi * (part.count - part.half), part.half, total * scale)

    spread[0:8] = jnp.zeros((8, 128), F32)
    unfold(3)
    loads["w", 0].wait()
    hs[...] = mm(taps[3], w[0:1152]).astype(BF)

    pl.semaphore_wait(barrier, 7 + jnp.where((sp == 3) | (sp == 4), 1, 0))
    halo = remote(hs, hr, edge_ss.at[0], edge_rs.at[0], above)
    slope_part = remote(ps, pr, edge_ss.at[1], edge_rs.at[1], below)
    slope_ct = remote(ct_hbm.at[pl.ds(0, 256)], cr, edge_ss.at[2], edge_rs.at[2], below)

    @pl.when(sp < 7)
    def _():
        halo.start()

    @pl.when(sp > 0)
    def _():
        slope_ct.start()

    for peer in near:
        signal(ready, peer)

    unfold(0)
    unfold(1)
    loads["w", 1].wait()
    loads["w", 2].wait()
    pre0 = mm(taps[0], w[1152:2304]) + mm(taps[1], w[2304:3456])
    ps[...] = pre0.astype(BF)

    @pl.when(sp > 0)
    def _():
        slope_part.start()

    turn(3)
    turn(1)
    turn(0)
    unfold(2)
    pre1 = mm(taps[1], w[0:1152]) + mm(taps[2], w[1152:2304]) + mm(taps[3], w[2304:3456])
    loads["c"].wait()
    finish(1, pre1)
    share(1).start()
    turn(2)
    to_right(1)

    @pl.when(sp > 0)
    def _():
        halo.wait_recv()

    finish(0, pre0 + hr[...].astype(F32))
    share(0).start()

    part1, part2 = own_part(1), own_part(2)
    for c in pairs:
        c.wait_recv()
    share(1).wait_recv()
    share(0).wait_recv()
    pl.semaphore_wait(ready, len(near))
    put(0, part1 + pair_part(1))
    put(1, part2 + pair_part(2))

    @pl.when(sp < 7)
    def _():
        slope_ct.wait_recv()
        slope_part.wait_recv()
        _, slope = slope_of(pr[...].astype(F32) + hs[...].astype(F32))
        gp[2] = (cr[...].astype(F32) * slope).astype(BF)

    share(2).start()
    part0 = own_part(0)
    grad_plane(2)
    share(2).wait_recv()
    total0 = part0 + pair_part(0)
    put(2, total0)
    put(3, total0)
    to_right(0)
    to_right(2)
    for p in (0, 1, 3):
        grad_plane(p)

    columns = pl.ds(pl.multiple_of(sp * 512, 512), 512)
    sw_ref[:, columns] = swb[pl.ds(pl.multiple_of(sp * 32, 32), 32)]
    step(0, 0)
    step(1, 0)
    step(2, 0)
    step(3, 0)
    switches = []
    for j, to in enumerate(slabs):
        rows = pl.ds(pl.multiple_of(to[1] * 32, 32), 32)
        switches.append(remote(swb.at[rows], sw_ref.at[:, columns], sw_ss.at[j], sw_rs.at[j], to))
        switches[-1].start()
    step(0, 1)
    step(1, 1)
    step(2, 1)
    step(3, 1)
    step(1, 2)
    step(3, 2)
    step(0, 2)
    step(2, 2)
    step(1, 3)
    step(3, 3)

    for c in switches:
        c.wait()
    for c in pairs:
        c.wait_send()
    for o in range(3):
        share(o).wait_send()
    for i, part in enumerate(PARTS):
        for stage in range(4 if part.order == "y" else 3):
            for c in copies(i, stage):
                c.wait_send()

    @pl.when(sp < 7)
    def _():
        halo.wait_send()

    @pl.when(sp > 0)
    def _():
        slope_ct.wait_send()
        slope_part.wait_send()


def deliver(*refs):
    ins, outs, sem = refs[:3], refs[3:6], refs[6]
    moves = [pltpu.make_async_copy(a, b, sem.at[i]) for i, (a, b) in enumerate(zip(ins, outs))]
    for move in moves:
        move.start()
    for move in moves:
        move.wait()


RESULTS = (((32, 4096), BF), ((4, 1024, 128), BF), ((216, 256), F32))


def body(volume, weights, cotangent):
    count = 16 * 16 * 16 * 16
    vmem = pltpu.VMEM
    dma = pltpu.SemaphoreType.DMA
    whole = pl.BlockSpec(memory_space=pltpu.VMEM)
    far = pl.BlockSpec(memory_space=pltpu.HBM)
    results = pl.pallas_call(
        functools.partial(kernel, 1.0 / count**0.5),
        out_shape=tuple(pltpu.VMEM(shape, dtype) for shape, dtype in RESULTS),
        in_specs=[far] * 3,
        out_specs=(whole, whole, whole),
        scratch_shapes=[
            vmem((4, 1024, 128), BF),
            vmem((3456, 256), BF),
            vmem((512, 256), BF),
            vmem((1040, 128), F32),
            vmem((4, 256, 1152), BF),
            vmem((2, 4, 576, 256), BF),
            vmem((4, 576, 256), BF),
            vmem((3, 256, 256), BF),
            vmem((3, 256, 256), BF),
            vmem((3, 256, 256), BF),
            vmem((256, 256), BF),
            vmem((256, 256), BF),
            vmem((256, 256), BF),
            vmem((256, 256), BF),
            vmem((256, 256), BF),
            vmem((256, 512), BF),
            vmem((16, 64, 128), F32),
            dma((8,)),
            dma((7,)),
            dma((7,)),
            dma((3,)),
            dma((3,)),
            dma((7,)),
            dma((7,)),
            dma((SUMS,)),
            dma((SUMS,)),
            pltpu.SemaphoreType.REGULAR,
            *[shape for part in PARTS for shape in part.scratch()],
        ],
        compiler_params=pltpu.CompilerParams(
            collective_id=0, has_side_effects=True, vmem_limit_bytes=40 * 2**20
        ),
        name="conv_step",
    )(
        *(
            pltpu.with_memory_space_constraint(value, pltpu.HBM)
            for value in (
                volume.reshape(4, 1024, 128),
                weights.reshape(3456, 256),
                cotangent.reshape(512, 256),
            )
        )
    )
    switched, volume_grad, kernel_grad = pl.pallas_call(
        deliver,
        out_shape=tuple(jax.ShapeDtypeStruct(shape, dtype) for shape, dtype in RESULTS),
        in_specs=[whole] * 3,
        out_specs=[far] * 3,
        scratch_shapes=[dma((3,))],
        compiler_params=pltpu.CompilerParams(vmem_limit_bytes=8 * 2**20),
        name="deliver",
    )(*results)
    return (
        switched[None],
        volume_grad.reshape(1, 4, 32, 32, 128),
        kernel_grad.reshape(3, 3, 3, 8, 256),
    )


def solution(mesh):
    in_specs = (P("dp", "space", None, None, None), P(), P("dp", "space", None, None, None))
    out_specs = (
        P("dp", "space", None),
        P("dp", "space", None, None, None),
        P(None, None, None, "dp", None),
    )
    return jax.shard_map(body, mesh=mesh, in_specs=in_specs, out_specs=out_specs, check_vma=False)
```

time: 43.8 us -> 38.4 us (0.88)
  local copies, waits for them, and re-layouts: 4.68 us -> 0 us
  Pallas kernels: 38.3 us -> 37.6 us
    unnamed x5 -> x0, local copies, waits for them, and re-layouts: 4.68 us -> none
    pallas_call x1 -> x2, Pallas kernels: 38.3 us -> 37.6 us  [the longest x1 36.5 us: body(): pl.pallas_call(functools.partial(kernel, 1.0 / count ** 0.5), out_shape=t...]
where the time goes in v2:
time: 38.4 us; the launch traced here: 38.3 us
  Pallas kernels  37.6 us (98%)
  between operations  0.64 us (2%)
    pallas_call x1, Pallas kernels, body(): pl.pallas_call(functools.partial(kernel, 1.0 / count ** 0.5), out_shape=t...  36.5 us
    pallas_call x1, Pallas kernels, body(): pl.pallas_call(deliver, out_shape=tuple((jax.ShapeDtypeStruct(shape, dtyp...  1.15 us

profile of v2, /device:TPU:0, one launch (start us, length us, event | category | flops | bytes accessed | tf_op | source)
XLA Modules:
  0.0 38.3 jit_solution(3814144903532372380)
XLA Ops:
  0.6 36.5 %conv_step.1 = (bf16[32,4096]{1,0:T(8,128)(2,1)S(1)}, bf16[4,1024,128]{2,1,0:T(8,128)(2,1)S(1)}, f32[216,256]{1,0:T(8,128)S(1)}) custom-call(bf16[4,1024,128]{2,1,0:T(8,128)(2,1)} %bitcast.7, bf16[3456,256]{1,0:T(8,128)(2,1)} %bitcast.6, bf16[512,256]{1,0:T(8,128)(2,1)} %bitcast.8), custom_call_target="tpu_custom_call" | custom-call | tf_op jit(solution)/shard_map/conv_step/pallas_call | solution.py:406
  37.1 1.1 %deliver.1 = (bf16[32,4096]{1,0:T(8,128)(2,1)}, bf16[4,1024,128]{2,1,0:T(8,128)(2,1)}, f32[216,256]{1,0:T(8,128)}) custom-call(bf16[32,4096]{1,0:T(8,128)(2,1)S(1)} %get-tuple-element.9.refs_0_, bf16[4,1024,128]{2,1,0:T(8,128)(2,1)S(1)} %get-tuple-element.10.refs_1_, f32[216,256]{1,0:T(8,128)S(1)} %get-tuple-element.11.refs_2_), custom_call_target="tpu_custom_call" | custom-call | tf_op jit(solution)/shard_map/deliver/pallas_call | solution.py:455

commit v3 on v2

--- a/solution.py
+++ b/solution.py
@@ -26,38 +26,41 @@
 class Part:
     def __init__(self, kd, low, count, order):
         self.kd, self.low, self.count, self.order = kd, low, count, order
-        self.half = (count + 1) // 2
         if order == "z":
+            self.axes, self.held, self.starts = "zyx", count, (0,)
             self.sizes = ((4, 2 * count), (2, count), (1, count))
         else:
-            self.sizes = ((4, 4 * self.half), (4, self.half), (1, self.half))
-        self.copies = 9 if order == "z" else 10
+            self.axes, self.held = "yzx", (count + 1) // 2
+            self.starts = (0, count - self.held)
+            self.sizes = ((4, 4 * self.held), (4, self.held), (1, self.held))
+        self.copies = (3, 3, 3 if order == "z" else 7)
 
     def scratch(self):
         shapes = []
-        for blocks, tiles in self.sizes:
+        for (blocks, tiles), copies in zip(self.sizes, self.copies):
             shapes.append(pltpu.VMEM((blocks, tiles, 16, 128), F32))
             shapes.append(pltpu.VMEM((blocks, tiles, 16, 128), BF))
-            shapes.append(pltpu.VMEM((3, tiles, 16, 128), BF))
-        if self.order == "y":
-            shapes += [pltpu.VMEM((self.half, 16, 128), F32)] * 2
+            shapes.append(pltpu.VMEM((copies, tiles, 16, 128), BF))
         return shapes
 
 
-PARTS = (Part(1, 0, 9, "z"), Part(2, 0, 9, "y"), Part(0, 0, 5, "z"), Part(0, 5, 4, "y"))
-SUMS = sum(part.copies for part in PARTS)
+PARTS = (Part(1, 0, 9, "z"), Part(2, 0, 9, "y"), Part(0, 0, 5, "z"), Part(0, 5, 4, "z"))
+ORDER = (
+    (0, 0), (1, 0), (2, 0), (3, 0), (0, 1), (1, 1), (2, 1), (3, 1), (0, 2), (2, 2), (3, 2), (1, 2),
+)
+SUMS = sum(sum(part.copies) for part in PARTS)
 
 
 def kernel(scale, vol_hbm, w_hbm, ct_hbm, sw_ref, vg_ref, kg_ref, *rest):
     (
-        vol, w, ct, spread, taps, tt, ttr, gp, gps, gpr, hs, hr, ps, pr, cr, swb, fine,
-        in_sem, pair_ss, pair_rs, edge_ss, edge_rs, sw_ss, sw_rs, sum_ss, sum_rs, ready,
-    ) = rest[:27]
-    rest, room, number = list(rest[27:]), {}, {}
+        vol, w, ct, spread, taps, tt, ttr, gp, gps, gpr, hs, hr, ps, pr, cr, swb, crossed, fine, vg,
+        in_sem, out_sem, pair_ss, pair_rs, edge_ss, edge_rs, sw_ss, sw_rs, sum_ss, sum_rs, ready,
+    ) = rest[:30]
+    rest, room, number = list(rest[30:]), {}, {}
     for i, part in enumerate(PARTS):
         count = len(part.scratch())
         room[i], rest = rest[:count], rest[count:]
-        number[i] = sum(p.copies for p in PARTS[:i])
+        number[i] = sum(sum(p.copies) for p in PARTS[:i])
 
     dp, sp = lax.axis_index("dp"), lax.axis_index("space")
     core, z, y, x = dp % 2, (dp // 2) % 4, (sp // 4) * 2 + dp // 8, sp % 4
@@ -163,7 +166,9 @@
     def finish(o, v):
         s, slope = slope_of(v)
         gp[o] = (ct[pl.ds(o * 256, 256)].astype(F32) * slope).astype(BF)
-        swb[:, o * 256 : (o + 1) * 256] = nt(unit, (v * s).astype(BF)).astype(BF)
+        swb[o] = nt(unit, (v * s).astype(BF)).astype(BF)
+
+    planes = []
 
     def grad_plane(p):
         for half, moves in ((0, ((1, 0),)), (1, ((2, 0), (0, 1)))):
@@ -182,7 +187,9 @@
             more = nt(jnp.concatenate(lhs_right, axis=1), jnp.concatenate(rhs_right, axis=1))
             fine[:, pl.ds(half * 32, 16, stride=2), :] = both[:, :128].reshape(16, 16, 128)
             fine[:, pl.ds(half * 32 + 1, 16, stride=2), :] = (both[:, 128:] + more).reshape(16, 16, 128)
-        vg_ref[p] = fine[...].reshape(1024, 128).astype(BF)
+        vg[p] = fine[...].reshape(1024, 128).astype(BF)
+        planes.append(pltpu.make_async_copy(vg.at[p], vg_ref.at[p], out_sem.at[p]))
+        planes[-1].start()
 
     def own_part(kd):
         (a, oa), (b, ob) = PAIRS[kd]
@@ -194,47 +201,46 @@
         lhs = jnp.concatenate([ttr[a], ttr[b]], axis=1)
         return mm(lhs, jnp.concatenate([gpr[oa], gpr[ob]], axis=0))
 
+    place = {"x": x, "y": y, "z": z}
+    across = [chip((x + j) % 4, (y + 2) % 4, z, core) for j in range(4)]
+
     def copies(i, stage):
         part, refs, out = PARTS[i], room[i], []
-        if stage == 3:
-            at = number[i] + 9
-            return [remote(refs[9], refs[10], sum_ss.at[at], sum_rs.at[at], along["y"][1])]
-        axis = ("zyx" if part.order == "z" else "yzx")[stage]
-        mine = {"z": z, "y": y, "x": 0}[axis]
-        blocks = part.sizes[stage][0]
-        for j in range(3):
+        axis, blocks = part.axes[stage], part.sizes[stage][0]
+        peers = along[axis] + (across if part.copies[stage] == 7 else [])
+        for j, to in enumerate(peers):
             at = number[i] + stage * 3 + j
-            src = refs[3 * stage + 1].at[(mine + j + 1) % blocks]
-            out.append(remote(src, refs[3 * stage + 2].at[j], sum_ss.at[at], sum_rs.at[at], along[axis][j]))
+            src = refs[3 * stage + 1].at[(place[axis] + j + 1) % blocks]
+            out.append(remote(src, refs[3 * stage + 2].at[j], sum_ss.at[at], sum_rs.at[at], to))
         return out
 
     def send(i, stage):
-        for c in copies(i, stage):
+        for c in reversed(copies(i, stage)):
             c.start()
 
     def put(i, total):
         part, refs = PARTS[i], room[i]
-
-        def store(block, tile_at, tile):
-            refs[0][block, tile_at] = tile
-            refs[1][block, tile_at] = tile.astype(BF)
-
         for t in range(part.count):
             for group in range(8):
                 at = (part.low + t) * 64 + group * 8
                 tile = jnp.concatenate([total[at : at + 8, :128], total[at : at + 8, 128:]], axis=0)
+                half = tile.astype(BF)
                 y_lo, to_z = group // 4, group % 4
-                if part.order == "z":
-                    store(to_z, y_lo * part.count + t, tile)
-                else:
-                    for upper in range(2):
-                        k = t - upper * (part.count - part.half)
-                        if 0 <= k < part.half:
-                            store(upper * 2 + y_lo, to_z * part.half + k, tile)
+                for n, start in enumerate(part.starts):
+                    k = t - start
+                    if not 0 <= k < part.held:
+                        continue
+                    if part.order == "z":
+                        block, where = to_z, y_lo * part.held + k
+                    else:
+                        block, where = n * 2 + y_lo, to_z * part.held + k
+                    refs[0][block, where] = tile
+                    refs[1][block, where] = half
         send(i, 0)
 
-    def write(part, start, count, value):
-        for t in range(count):
+    def write(part, start, value):
+        value = value * scale
+        for t in range(part.held):
             at = pl.multiple_of((part.kd * 9 + part.low + start + t) * 8, 8)
             kg_ref[pl.ds(at, 8), 0:128] = value[t, 0:8]
             kg_ref[pl.ds(at, 8), 128:256] = value[t, 8:16]
@@ -243,13 +249,8 @@
         part, refs = PARTS[i], room[i]
         for c in copies(i, stage):
             c.wait_recv()
-        if stage == 3:
-            write(part, (1 - y_hi) * (part.count - part.half), part.half, refs[10][...])
-            return
         own, _, got = refs[3 * stage : 3 * stage + 3]
-        axis = ("zyx" if part.order == "z" else "yzx")[stage]
-        mine = {"z": z, "y": y, "x": 0}[axis]
-        total = own[mine % part.sizes[stage][0]]
+        total = own[place[part.axes[stage]] % part.sizes[stage][0]]
         for j in range(3):
             total = total + got[j].astype(F32)
         if stage < 2:
@@ -258,11 +259,43 @@
             refs[3 * stage + 4][...] = total.astype(BF)
             send(i, stage + 1)
         elif part.order == "z":
-            write(part, 0, part.count, total * scale)
+            write(part, 0, total)
         else:
-            refs[9][...] = total * scale
-            send(i, 3)
-            write(part, y_hi * (part.count - part.half), part.half, total * scale)
+            other = got[3].astype(F32)
+            for j in (4, 5, 6):
+                other = other + got[j].astype(F32)
+            write(part, y_hi * part.starts[1], total)
+            write(part, (1 - y_hi) * part.starts[1], other)
+
+    other_row = along["y"][1]
+    switches, locals_, crossings = [], [], []
+
+    def cells(slab, o):
+        return pl.ds(pl.multiple_of(slab * 512 + o * 256, 256), 256)
+
+    def hand_out(at, rows_of, slab, o):
+        for j in range(4):
+            rows = pl.ds(pl.multiple_of((x + j) % 4 * 32, 32), 32)
+            src, dst = rows_of.at[rows], sw_ref.at[:, cells(slab, o)]
+            if j == 0:
+                locals_.append(pltpu.make_async_copy(src, dst, out_sem.at[4 + at // 3]))
+                locals_[-1].start()
+            else:
+                k = at + j - 1
+                switches.append(remote(src, dst, sw_ss.at[k], sw_rs.at[k], along["x"][j - 1]))
+                switches[-1].start()
+
+    def switch(o):
+        rows = pl.ds(pl.multiple_of((1 - y_hi) * 128, 128), 128)
+        crossings.append(remote(swb.at[o, rows], crossed.at[o], sw_ss.at[12 + o], sw_rs.at[12 + o], other_row))
+        crossings[-1].start()
+        rows = pl.ds(pl.multiple_of(y_hi * 128, 128), 128)
+        hand_out(o * 3, swb.at[o, rows], sp, o)
+
+    def switch_on():
+        for o, crossing in zip((1, 0), crossings):
+            crossing.wait_recv()
+            hand_out(6 + o * 3, crossed.at[o], (1 - y_hi) * 4 + x, o)
 
     spread[0:8] = jnp.zeros((8, 128), F32)
     unfold(3)
@@ -300,11 +333,13 @@
     turn(1)
     turn(0)
     unfold(2)
+    turn(2)
     pre1 = mm(taps[1], w[0:1152]) + mm(taps[2], w[1152:2304]) + mm(taps[3], w[2304:3456])
     loads["c"].wait()
     finish(1, pre1)
     share(1).start()
-    turn(2)
+    pl.semaphore_wait(ready, len(near))
+    switch(1)
     to_right(1)
 
     @pl.when(sp > 0)
@@ -313,13 +348,13 @@
 
     finish(0, pre0 + hr[...].astype(F32))
     share(0).start()
+    switch(0)
 
     part1, part2 = own_part(1), own_part(2)
     for c in pairs:
         c.wait_recv()
     share(1).wait_recv()
     share(0).wait_recv()
-    pl.semaphore_wait(ready, len(near))
     put(0, part1 + pair_part(1))
     put(1, part2 + pair_part(2))
 
@@ -339,31 +374,17 @@
     put(3, total0)
     to_right(0)
     to_right(2)
+    switch_on()
     for p in (0, 1, 3):
         grad_plane(p)
 
-    columns = pl.ds(pl.multiple_of(sp * 512, 512), 512)
-    sw_ref[:, columns] = swb[pl.ds(pl.multiple_of(sp * 32, 32), 32)]
-    step(0, 0)
-    step(1, 0)
-    step(2, 0)
-    step(3, 0)
-    switches = []
-    for j, to in enumerate(slabs):
-        rows = pl.ds(pl.multiple_of(to[1] * 32, 32), 32)
-        switches.append(remote(swb.at[rows], sw_ref.at[:, columns], sw_ss.at[j], sw_rs.at[j], to))
-        switches[-1].start()
-    step(0, 1)
-    step(1, 1)
-    step(2, 1)
-    step(3, 1)
-    step(1, 2)
-    step(3, 2)
-    step(0, 2)
-    step(2, 2)
-    step(1, 3)
-    step(3, 3)
-
+    for i, stage in ORDER:
+        step(i, stage)
+
+    for c in planes + locals_:
+        c.wait()
+    for c in crossings:
+        c.wait_send()
     for c in switches:
         c.wait()
     for c in pairs:
@@ -371,7 +392,7 @@
     for o in range(3):
         share(o).wait_send()
     for i, part in enumerate(PARTS):
-        for stage in range(4 if part.order == "y" else 3):
+        for stage in range(3):
             for c in copies(i, stage):
                 c.wait_send()
 
@@ -403,11 +424,12 @@
     dma = pltpu.SemaphoreType.DMA
     whole = pl.BlockSpec(memory_space=pltpu.VMEM)
     far = pl.BlockSpec(memory_space=pltpu.HBM)
+    anywhere = pl.BlockSpec(memory_space=pl.ANY)
     results = pl.pallas_call(
         functools.partial(kernel, 1.0 / count**0.5),
         out_shape=tuple(pltpu.VMEM(shape, dtype) for shape, dtype in RESULTS),
         in_specs=[far] * 3,
-        out_specs=(whole, whole, whole),
+        out_specs=(anywhere, anywhere, whole),
         scratch_shapes=[
             vmem((4, 1024, 128), BF),
             vmem((3456, 256), BF),
@@ -424,15 +446,18 @@
             vmem((256, 256), BF),
             vmem((256, 256), BF),
             vmem((256, 256), BF),
-            vmem((256, 512), BF),
+            vmem((2, 256, 256), BF),
+            vmem((2, 128, 256), BF),
             vmem((16, 64, 128), F32),
+            vmem((4, 1024, 128), BF),
+            dma((8,)),
             dma((8,)),
             dma((7,)),
             dma((7,)),
             dma((3,)),
             dma((3,)),
-            dma((7,)),
-            dma((7,)),
+            dma((14,)),
+            dma((14,)),
             dma((SUMS,)),
             dma((SUMS,)),
             pltpu.SemaphoreType.REGULAR,
@@ -455,7 +480,7 @@
     switched, volume_grad, kernel_grad = pl.pallas_call(
         deliver,
         out_shape=tuple(jax.ShapeDtypeStruct(shape, dtype) for shape, dtype in RESULTS),
-        in_specs=[whole] * 3,
+        in_specs=[anywhere] * 3,
         out_specs=[far] * 3,
         scratch_shapes=[dma((3,))],
         compiler_params=pltpu.CompilerParams(vmem_limit_bytes=8 * 2**20),

time: 38.4 us -> 35.6 us (0.927)
  the two profiles are of different devices: /device:TPU:0 before, /device:TPU:1 now
where the time goes in v3:
time: 35.6 us; the launch traced here: 35.5 us
  Pallas kernels  34.8 us (98%)
  between operations  0.64 us (2%)
    pallas_call x1, Pallas kernels, body(): pl.pallas_call(functools.partial(kernel, 1.0 / count ** 0.5), out_shape=t...  33.7 us
    pallas_call x1, Pallas kernels, body(): pl.pallas_call(deliver, out_shape=tuple((jax.ShapeDtypeStruct(shape, dtyp...  1.15 us

profile of v3, /device:TPU:1, one launch (start us, length us, event | category | flops | bytes accessed | tf_op | source)
XLA Modules:
  0.0 35.5 jit_solution(13123291450472665905)
XLA Ops:
  0.6 33.7 %conv_step.1 = (bf16[32,4096]{1,0:T(8,128)(2,1)S(1)}, bf16[4,1024,128]{2,1,0:T(8,128)(2,1)S(1)}, f32[216,256]{1,0:T(8,128)S(1)}) custom-call(bf16[4,1024,128]{2,1,0:T(8,128)(2,1)} %bitcast.7, bf16[3456,256]{1,0:T(8,128)(2,1)} %bitcast.6, bf16[512,256]{1,0:T(8,128)(2,1)} %bitcast.8), custom_call_target="tpu_custom_call" | custom-call | tf_op jit(solution)/shard_map/conv_step/pallas_call | solution.py:428
  34.3 1.1 %deliver.1 = (bf16[32,4096]{1,0:T(8,128)(2,1)}, bf16[4,1024,128]{2,1,0:T(8,128)(2,1)}, f32[216,256]{1,0:T(8,128)}) custom-call(bf16[32,4096]{1,0:T(8,128)(2,1)S(1)} %get-tuple-element.9.refs_0_, bf16[4,1024,128]{2,1,0:T(8,128)(2,1)S(1)} %get-tuple-element.10.refs_1_, f32[216,256]{1,0:T(8,128)S(1)} %get-tuple-element.11.refs_2_), custom_call_target="tpu_custom_call" | custom-call | tf_op jit(solution)/shard_map/deliver/pallas_call | solution.py:480

commit v4 on v3

--- a/solution.py
+++ b/solution.py
@@ -26,14 +26,24 @@
 class Part:
     def __init__(self, kd, low, count, order):
         self.kd, self.low, self.count, self.order = kd, low, count, order
-        if order == "z":
-            self.axes, self.held, self.starts = "zyx", count, (0,)
+        self.axes, self.first = order, order[0]
+        self.held, self.starts = count, (0,)
+        self.copies, self.gathered = (3, 3, 3), False
+        if order == "zyx":
             self.sizes = ((4, 2 * count), (2, count), (1, count))
-        else:
-            self.axes, self.held = "yzx", (count + 1) // 2
+        elif order == "zxy":
+            self.sizes = ((4, 2 * count), (1, 2 * count), (2, count))
+        elif order[0] == "y":
+            self.held = (count + 1) // 2
             self.starts = (0, count - self.held)
             self.sizes = ((4, 4 * self.held), (4, self.held), (1, self.held))
-        self.copies = (3, 3, 3 if order == "z" else 7)
+            self.copies = (3, 3, 7 if order == "yzx" else 3)
+            self.gathered = order == "yzxy"
+        else:
+            self.held = (count + 3) // 4
+            self.starts = tuple((count - self.held) * i // 3 for i in range(4))
+            self.sizes = ((4, 8 * self.held), (4, 2 * self.held), (2, self.held))
+            self.gathered = True
 
     def scratch(self):
         shapes = []
@@ -41,26 +51,27 @@
             shapes.append(pltpu.VMEM((blocks, tiles, 16, 128), F32))
             shapes.append(pltpu.VMEM((blocks, tiles, 16, 128), BF))
             shapes.append(pltpu.VMEM((copies, tiles, 16, 128), BF))
+        if self.gathered:
+            shapes.append(pltpu.VMEM((self.held, 16, 128), F32))
+            shapes.append(pltpu.VMEM((3 if self.first == "x" else 1, self.held, 16, 128), F32))
         return shapes
 
 
-PARTS = (Part(1, 0, 9, "z"), Part(2, 0, 9, "y"), Part(0, 0, 5, "z"), Part(0, 5, 4, "z"))
-ORDER = (
-    (0, 0), (1, 0), (2, 0), (3, 0), (0, 1), (1, 1), (2, 1), (3, 1), (0, 2), (2, 2), (3, 2), (1, 2),
-)
-SUMS = sum(sum(part.copies) for part in PARTS)
+PARTS = (Part(1, 0, 9, "zyx"), Part(2, 0, 9, "yzx"), Part(0, 0, 5, "zyx"), Part(0, 5, 4, "yzx"),)
+ORDER = ((0, 0), (1, 0), (2, 0), (3, 0), (0, 1), (1, 1), (2, 1), (3, 1), (0, 2), (2, 2), (3, 2), (1, 2))
+DURING = {(0, 0): 0, (2, 0): 1, (0, 2): 3}
+SUMS = 4 * len(PARTS)
 
 
 def kernel(scale, vol_hbm, w_hbm, ct_hbm, sw_ref, vg_ref, kg_ref, *rest):
     (
-        vol, w, ct, spread, taps, tt, ttr, gp, gps, gpr, hs, hr, ps, pr, cr, swb, crossed, fine, vg,
+        vol, w, ct, spread, taps, tt, ttr, gp, gps, gpr, hs, hr, ps, pr, cr, swb, crossed, fine, vg, own,
         in_sem, out_sem, pair_ss, pair_rs, edge_ss, edge_rs, sw_ss, sw_rs, sum_ss, sum_rs, ready,
-    ) = rest[:30]
-    rest, room, number = list(rest[30:]), {}, {}
+    ) = rest[:31]
+    rest, room = list(rest[31:]), {}
     for i, part in enumerate(PARTS):
         count = len(part.scratch())
         room[i], rest = rest[:count], rest[count:]
-        number[i] = sum(sum(p.copies) for p in PARTS[:i])
 
     dp, sp = lax.axis_index("dp"), lax.axis_index("space")
     core, z, y, x = dp % 2, (dp // 2) % 4, (sp // 4) * 2 + dp // 8, sp % 4
@@ -85,6 +96,22 @@
 
     def signal(sem, to):
         pl.semaphore_signal(sem, inc=1, device_id=to, device_id_type=MESH)
+
+    def landed(ref, sem):
+        pltpu.make_async_copy(ref, ref, sem).wait()
+
+    barrier = pltpu.get_barrier_semaphore()
+    near = [along[axis][j] for axis in "xyz" for j in (0, 2)]
+    for peer in [partner, *near]:
+        signal(barrier, peer)
+
+    @pl.when(sp == 3)
+    def _():
+        signal(barrier, above)
+
+    @pl.when(sp == 4)
+    def _():
+        signal(barrier, below)
 
     loads = {}
     for i, p in enumerate((3, 0, 1, 2)):
@@ -95,19 +122,6 @@
     loads["c"] = pltpu.make_async_copy(ct_hbm, ct, in_sem.at[7])
     for which in (("v", 3), ("w", 0), ("v", 0), ("v", 1), ("w", 1), ("w", 2), ("v", 2), "c"):
         loads[which].start()
-
-    barrier = pltpu.get_barrier_semaphore()
-    near = [along[axis][j] for axis in "xyz" for j in (0, 2)]
-    for peer in [partner, *near]:
-        signal(barrier, peer)
-
-    @pl.when(sp == 3)
-    def _():
-        signal(barrier, above)
-
-    @pl.when(sp == 4)
-    def _():
-        signal(barrier, below)
 
     def edge(condition, ref):
         @pl.when(condition)
@@ -138,22 +152,20 @@
     column = lax.broadcasted_iota(jnp.int32, (128, 128), 1)
     channel = (((row % 64) // 8) * 2 + row // 64) * 8 + row % 8
     sort = (column == channel).astype(F32).astype(BF)
-    pairs = []
 
     def turn(p):
         for t in range(TAPS):
             turned = nt(sort, taps[p, :, t * 128 : (t + 1) * 128]).astype(BF)
             tt[0, p, t * 64 : (t + 1) * 64] = turned[:64]
             tt[1, p, t * 64 : (t + 1) * 64] = turned[64:]
-        pairs.append(remote(tt.at[1 - core, p], ttr.at[p], pair_ss.at[p], pair_rs.at[p], partner))
-        pairs[-1].start()
+        remote(tt.at[1 - core, p], ttr.at[p], pair_ss.at[3], pair_rs.at[3], partner).start()
 
     er = lax.broadcasted_iota(jnp.int32, (256, 256), 0)
     ec = lax.broadcasted_iota(jnp.int32, (256, 256), 1)
     unit = (er == ec).astype(F32).astype(BF)
 
     def share(o):
-        return remote(gp.at[o], gpr.at[o], pair_ss.at[4 + o], pair_rs.at[4 + o], partner)
+        return remote(gp.at[o], gpr.at[o], pair_ss.at[o], pair_rs.at[o], partner)
 
     def to_right(o):
         value = gp[o].astype(F32)
@@ -167,8 +179,6 @@
         s, slope = slope_of(v)
         gp[o] = (ct[pl.ds(o * 256, 256)].astype(F32) * slope).astype(BF)
         swb[o] = nt(unit, (v * s).astype(BF)).astype(BF)
-
-    planes = []
 
     def grad_plane(p):
         for half, moves in ((0, ((1, 0),)), (1, ((2, 0), (0, 1)))):
@@ -188,13 +198,12 @@
             fine[:, pl.ds(half * 32, 16, stride=2), :] = both[:, :128].reshape(16, 16, 128)
             fine[:, pl.ds(half * 32 + 1, 16, stride=2), :] = (both[:, 128:] + more).reshape(16, 16, 128)
         vg[p] = fine[...].reshape(1024, 128).astype(BF)
-        planes.append(pltpu.make_async_copy(vg.at[p], vg_ref.at[p], out_sem.at[p]))
-        planes[-1].start()
+        pltpu.make_async_copy(vg.at[p], vg_ref.at[p], out_sem.at[0]).start()
 
     def own_part(kd):
         (a, oa), (b, ob) = PAIRS[kd]
         lhs = jnp.concatenate([tt[core, a], tt[core, b]], axis=1)
-        return mm(lhs, jnp.concatenate([gp[oa], gp[ob]], axis=0))
+        own[kd] = mm(lhs, jnp.concatenate([gp[oa], gp[ob]], axis=0))
 
     def pair_part(kd):
         (a, oa), (b, ob) = PAIRS[kd]
@@ -206,13 +215,21 @@
 
     def copies(i, stage):
         part, refs, out = PARTS[i], room[i], []
+        at = i * 4 + stage
+        if stage == 3:
+            return [
+                remote(refs[9], refs[10].at[j], sum_ss.at[at], sum_rs.at[at], to)
+                for j, to in enumerate(along["x"] if part.first == "x" else along["y"][1:2])
+            ]
         axis, blocks = part.axes[stage], part.sizes[stage][0]
         peers = along[axis] + (across if part.copies[stage] == 7 else [])
         for j, to in enumerate(peers):
-            at = number[i] + stage * 3 + j
             src = refs[3 * stage + 1].at[(place[axis] + j + 1) % blocks]
             out.append(remote(src, refs[3 * stage + 2].at[j], sum_ss.at[at], sum_rs.at[at], to))
         return out
+
+    def arrived(i, stage, sems):
+        landed(room[i][10 if stage == 3 else 3 * stage + 2], sems.at[i * 4 + stage])
 
     def send(i, stage):
         for c in reversed(copies(i, stage)):
@@ -230,27 +247,41 @@
                     k = t - start
                     if not 0 <= k < part.held:
                         continue
-                    if part.order == "z":
+                    if part.first == "z":
                         block, where = to_z, y_lo * part.held + k
+                    elif part.first == "y":
+                        block, where = n * 2 + y_lo, to_z * part.held + k
                     else:
-                        block, where = n * 2 + y_lo, to_z * part.held + k
+                        block, where = n, (to_z * 2 + y_lo) * part.held + k
                     refs[0][block, where] = tile
                     refs[1][block, where] = half
         send(i, 0)
 
-    def write(part, start, value):
+    def put_all(kd, total):
+        for i, part in enumerate(PARTS):
+            if part.kd == kd:
+                put(i, total)
+
+    def write(part, owner, value):
+        stride = part.starts[1] if len(part.starts) > 1 else 0
         value = value * scale
         for t in range(part.held):
-            at = pl.multiple_of((part.kd * 9 + part.low + start + t) * 8, 8)
+            at = pl.multiple_of((part.kd * 9 + part.low + owner * stride + t) * 8, 8)
             kg_ref[pl.ds(at, 8), 0:128] = value[t, 0:8]
             kg_ref[pl.ds(at, 8), 128:256] = value[t, 8:16]
 
     def step(i, stage):
         part, refs = PARTS[i], room[i]
-        for c in copies(i, stage):
-            c.wait_recv()
-        own, _, got = refs[3 * stage : 3 * stage + 3]
-        total = own[place[part.axes[stage]] % part.sizes[stage][0]]
+        arrived(i, stage, sum_rs)
+        if stage == 3:
+            if part.first == "y":
+                write(part, 1 - y_hi, refs[10][0])
+            else:
+                for j in range(3):
+                    write(part, (x + 3 - j) % 4, refs[10][j])
+            return
+        kept, _, got = refs[3 * stage : 3 * stage + 3]
+        total = kept[place[part.axes[stage]] % part.sizes[stage][0]]
         for j in range(3):
             total = total + got[j].astype(F32)
         if stage < 2:
@@ -258,44 +289,43 @@
             refs[3 * stage + 3][...] = total
             refs[3 * stage + 4][...] = total.astype(BF)
             send(i, stage + 1)
-        elif part.order == "z":
-            write(part, 0, total)
-        else:
+            return
+        if part.gathered:
+            refs[9][...] = total
+            send(i, 3)
+        write(part, {"z": 0, "y": y_hi, "x": x}[part.first], total)
+        if part.copies[2] == 7:
             other = got[3].astype(F32)
             for j in (4, 5, 6):
                 other = other + got[j].astype(F32)
-            write(part, y_hi * part.starts[1], total)
-            write(part, (1 - y_hi) * part.starts[1], other)
+            write(part, 1 - y_hi, other)
 
     other_row = along["y"][1]
-    switches, locals_, crossings = [], [], []
+    crossings = []
 
     def cells(slab, o):
         return pl.ds(pl.multiple_of(slab * 512 + o * 256, 256), 256)
 
-    def hand_out(at, rows_of, slab, o):
+    def hand_out(rows_of, slab, o):
         for j in range(4):
             rows = pl.ds(pl.multiple_of((x + j) % 4 * 32, 32), 32)
             src, dst = rows_of.at[rows], sw_ref.at[:, cells(slab, o)]
             if j == 0:
-                locals_.append(pltpu.make_async_copy(src, dst, out_sem.at[4 + at // 3]))
-                locals_[-1].start()
+                pltpu.make_async_copy(src, dst, out_sem.at[1]).start()
             else:
-                k = at + j - 1
-                switches.append(remote(src, dst, sw_ss.at[k], sw_rs.at[k], along["x"][j - 1]))
-                switches[-1].start()
+                remote(src, dst, sw_ss.at[2], sw_rs.at[2], along["x"][j - 1]).start()
 
     def switch(o):
         rows = pl.ds(pl.multiple_of((1 - y_hi) * 128, 128), 128)
-        crossings.append(remote(swb.at[o, rows], crossed.at[o], sw_ss.at[12 + o], sw_rs.at[12 + o], other_row))
+        crossings.append(remote(swb.at[o, rows], crossed.at[o], sw_ss.at[o], sw_rs.at[o], other_row))
         crossings[-1].start()
         rows = pl.ds(pl.multiple_of(y_hi * 128, 128), 128)
-        hand_out(o * 3, swb.at[o, rows], sp, o)
+        hand_out(swb.at[o, rows], sp, o)
 
     def switch_on():
         for o, crossing in zip((1, 0), crossings):
             crossing.wait_recv()
-            hand_out(6 + o * 3, crossed.at[o], (1 - y_hi) * 4 + x, o)
+            hand_out(crossed.at[o], (1 - y_hi) * 4 + x, o)
 
     spread[0:8] = jnp.zeros((8, 128), F32)
     unfold(3)
@@ -350,13 +380,15 @@
     share(0).start()
     switch(0)
 
-    part1, part2 = own_part(1), own_part(2)
-    for c in pairs:
-        c.wait_recv()
+    own_part(1)
+    own_part(2)
+    landed(ttr, pair_rs.at[3])
     share(1).wait_recv()
     share(0).wait_recv()
-    put(0, part1 + pair_part(1))
-    put(1, part2 + pair_part(2))
+    total1 = own[1] + pair_part(1)
+    put_all(1, total1)
+    total2 = own[2] + pair_part(2)
+    put_all(2, total2)
 
     @pl.when(sp < 7)
     def _():
@@ -366,35 +398,30 @@
         gp[2] = (cr[...].astype(F32) * slope).astype(BF)
 
     share(2).start()
-    part0 = own_part(0)
+    own_part(0)
     grad_plane(2)
     share(2).wait_recv()
-    total0 = part0 + pair_part(0)
-    put(2, total0)
-    put(3, total0)
+    total0 = own[0] + pair_part(0)
+    put_all(0, total0)
     to_right(0)
     to_right(2)
     switch_on()
-    for p in (0, 1, 3):
-        grad_plane(p)
-
     for i, stage in ORDER:
+        if (i, stage) in DURING:
+            grad_plane(DURING[i, stage])
         step(i, stage)
 
-    for c in planes + locals_:
-        c.wait()
+    landed(vg, out_sem.at[0])
+    landed(sw_ref.at[:, pl.ds(0, 1024)], out_sem.at[1])
+    landed(sw_ref.at[:, pl.ds(0, 3072)], sw_rs.at[2])
+    landed(sw_ref.at[:, pl.ds(0, 3072)], sw_ss.at[2])
     for c in crossings:
         c.wait_send()
-    for c in switches:
-        c.wait()
-    for c in pairs:
-        c.wait_send()
+    landed(ttr, pair_ss.at[3])
     for o in range(3):
         share(o).wait_send()
-    for i, part in enumerate(PARTS):
-        for stage in range(3):
-            for c in copies(i, stage):
-                c.wait_send()
+    for i, stage in ORDER:
+        arrived(i, stage, sum_ss)
 
     @pl.when(sp < 7)
     def _():
@@ -406,9 +433,10 @@
         slope_part.wait_send()
 
 
-def deliver(*refs):
-    ins, outs, sem = refs[:3], refs[3:6], refs[6]
-    moves = [pltpu.make_async_copy(a, b, sem.at[i]) for i, (a, b) in enumerate(zip(ins, outs))]
+def deliver(sw_in, vg_in, kg_in, sw_out, vg_out, kg_out, sem):
+    moves = [(kg_in, kg_out), (sw_in, sw_out)]
+    moves += [(vg_in.at[p], vg_out.at[p]) for p in range(4)]
+    moves = [pltpu.make_async_copy(a, b, sem.at[i]) for i, (a, b) in enumerate(moves)]
     for move in moves:
         move.start()
     for move in moves:
@@ -450,14 +478,15 @@
             vmem((2, 128, 256), BF),
             vmem((16, 64, 128), F32),
             vmem((4, 1024, 128), BF),
+            vmem((3, 576, 256), F32),
             dma((8,)),
-            dma((8,)),
-            dma((7,)),
-            dma((7,)),
+            dma((2,)),
+            dma((4,)),
+            dma((4,)),
             dma((3,)),
             dma((3,)),
-            dma((14,)),
-            dma((14,)),
+            dma((3,)),
+            dma((3,)),
             dma((SUMS,)),
             dma((SUMS,)),
             pltpu.SemaphoreType.REGULAR,
@@ -482,7 +511,7 @@
         out_shape=tuple(jax.ShapeDtypeStruct(shape, dtype) for shape, dtype in RESULTS),
         in_specs=[anywhere] * 3,
         out_specs=[far] * 3,
-        scratch_shapes=[dma((3,))],
+        scratch_shapes=[dma((6,))],
         compiler_params=pltpu.CompilerParams(vmem_limit_bytes=8 * 2**20),
         name="deliver",
     )(*results)

time: 35.6 us -> 34 us (0.955)
  the two profiles are of different devices: /device:TPU:1 before, /device:TPU:0 now
where the time goes in v4:
time: 34 us; the launch traced here: 33.6 us
  Pallas kernels  33 us (97%)
  between operations  0.64 us (2%)
    pallas_call x1, Pallas kernels, body(): pl.pallas_call(functools.partial(kernel, 1.0 / count ** 0.5), out_shape=t...  31.8 us
    pallas_call x1, Pallas kernels, body(): pl.pallas_call(deliver, out_shape=tuple((jax.ShapeDtypeStruct(shape, dtyp...  1.17 us

profile of v4, /device:TPU:0, one launch (start us, length us, event | category | flops | bytes accessed | tf_op | source)
XLA Modules:
  0.0 33.6 jit_solution(8796164787864423595)
XLA Ops:
  0.6 31.8 %conv_step.1 = (bf16[32,4096]{1,0:T(8,128)(2,1)S(1)}, bf16[4,1024,128]{2,1,0:T(8,128)(2,1)S(1)}, f32[216,256]{1,0:T(8,128)S(1)}) custom-call(bf16[4,1024,128]{2,1,0:T(8,128)(2,1)} %bitcast.7, bf16[3456,256]{1,0:T(8,128)(2,1)} %bitcast.6, bf16[512,256]{1,0:T(8,128)(2,1)} %bitcast.8), custom_call_target="tpu_custom_call" | custom-call | tf_op jit(solution)/shard_map/conv_step/pallas_call | solution.py:456
  32.4 1.2 %deliver.1 = (bf16[32,4096]{1,0:T(8,128)(2,1)}, bf16[4,1024,128]{2,1,0:T(8,128)(2,1)}, f32[216,256]{1,0:T(8,128)}) custom-call(bf16[32,4096]{1,0:T(8,128)(2,1)S(1)} %get-tuple-element.9.sw_in, bf16[4,1024,128]{2,1,0:T(8,128)(2,1)S(1)} %get-tuple-element.10.vg_in, f32[216,256]{1,0:T(8,128)S(1)} %get-tuple-element.11.kg_in), custom_call_target="tpu_custom_call" | custom-call | tf_op jit(solution)/shard_map/deliver/pallas_call | solution.py:509

commit v5 on v4

--- a/solution.py
+++ b/solution.py
@@ -59,7 +59,7 @@
 
 PARTS = (Part(1, 0, 9, "zyx"), Part(2, 0, 9, "yzx"), Part(0, 0, 5, "zyx"), Part(0, 5, 4, "yzx"),)
 ORDER = ((0, 0), (1, 0), (2, 0), (3, 0), (0, 1), (1, 1), (2, 1), (3, 1), (0, 2), (2, 2), (3, 2), (1, 2))
-DURING = {(0, 0): 0, (2, 0): 1, (0, 2): 3}
+DURING = {(0, 0): 0, (1, 0): 1, (0, 2): 3}
 SUMS = 4 * len(PARTS)
 
 
@@ -197,7 +197,7 @@
             more = nt(jnp.concatenate(lhs_right, axis=1), jnp.concatenate(rhs_right, axis=1))
             fine[:, pl.ds(half * 32, 16, stride=2), :] = both[:, :128].reshape(16, 16, 128)
             fine[:, pl.ds(half * 32 + 1, 16, stride=2), :] = (both[:, 128:] + more).reshape(16, 16, 128)
-        vg[p] = fine[...].reshape(1024, 128).astype(BF)
+        vg[p] = fine[:, 0:64].reshape(1024, 128).astype(BF)
         pltpu.make_async_copy(vg.at[p], vg_ref.at[p], out_sem.at[0]).start()
 
     def own_part(kd):
@@ -405,11 +405,12 @@
     put_all(0, total0)
     to_right(0)
     to_right(2)
-    switch_on()
     for i, stage in ORDER:
         if (i, stage) in DURING:
             grad_plane(DURING[i, stage])
         step(i, stage)
+        if (i, stage) == (0, 0):
+            switch_on()
 
     landed(vg, out_sem.at[0])
     landed(sw_ref.at[:, pl.ds(0, 1024)], out_sem.at[1])
@@ -476,7 +477,7 @@
             vmem((256, 256), BF),
             vmem((2, 256, 256), BF),
             vmem((2, 128, 256), BF),
-            vmem((16, 64, 128), F32),
+            vmem((16, 72, 128), F32),
             vmem((4, 1024, 128), BF),
             vmem((3, 576, 256), F32),
             dma((8,)),

time: 34 us -> 34 us (level)
  no operation moved by 1% of the time
where the time goes in v5:
time: 34 us; the launch traced here: 33.6 us
  Pallas kernels  33 us (97%)
  between operations  0.64 us (2%)
    pallas_call x1, Pallas kernels, body(): pl.pallas_call(functools.partial(kernel, 1.0 / count ** 0.5), out_shape=t...  31.8 us
    pallas_call x1, Pallas kernels, body(): pl.pallas_call(deliver, out_shape=tuple((jax.ShapeDtypeStruct(shape, dtyp...  1.17 us

profile of v5, /device:TPU:0, one launch (start us, length us, event | category | flops | bytes accessed | tf_op | source)
XLA Modules:
  0.0 33.6 jit_solution(8224756348897889171)
XLA Ops:
  0.6 31.8 %conv_step.1 = (bf16[32,4096]{1,0:T(8,128)(2,1)S(1)}, bf16[4,1024,128]{2,1,0:T(8,128)(2,1)S(1)}, f32[216,256]{1,0:T(8,128)S(1)}) custom-call(bf16[4,1024,128]{2,1,0:T(8,128)(2,1)} %bitcast.7, bf16[3456,256]{1,0:T(8,128)(2,1)} %bitcast.6, bf16[512,256]{1,0:T(8,128)(2,1)} %bitcast.8), custom_call_target="tpu_custom_call" | custom-call | tf_op jit(solution)/shard_map/conv_step/pallas_call | solution.py:457
  32.4 1.2 %deliver.1 = (bf16[32,4096]{1,0:T(8,128)(2,1)}, bf16[4,1024,128]{2,1,0:T(8,128)(2,1)}, f32[216,256]{1,0:T(8,128)}) custom-call(bf16[32,4096]{1,0:T(8,128)(2,1)S(1)} %get-tuple-element.9.sw_in, bf16[4,1024,128]{2,1,0:T(8,128)(2,1)S(1)} %get-tuple-element.10.vg_in, f32[216,256]{1,0:T(8,128)S(1)} %get-tuple-element.11.kg_in), custom_call_target="tpu_custom_call" | custom-call | tf_op jit(solution)/shard_map/deliver/pallas_call | solution.py:510
